TPU v7x, 32 devices: a whole 2x2x4 slice. The times are simulated.
32 devices in a mesh: dp: 8 (over y, x, core), tensor: 4 (over z).
Axes of the slice: x: 2, y: 2, z: 4, core: 2. Of those that a mesh axis runs over, the one named last changes fastest.
Arguments:
- tokens: bfloat16 [512, 8192], P('dp'), may hold values from -6 to 6
- gate_weight: bfloat16 [8192, 14848], P('dp', 'tensor'), may hold values from -0.09375 to 0.09375
- up_weight: bfloat16 [8192, 14848], P('dp', 'tensor'), may hold values from -0.09375 to 0.09375
- down_weight: bfloat16 [14848, 8192], P('tensor', 'dp'), may hold values from -6 to 6
- channel_group: int32 [14848], P('tensor'), may hold values from 0 to 115, as said below
- owners: int32 [116], replicated, may hold values from 0 to 3
Outputs:
- group_scores: float32 [4, 116], P('tensor')
Inputs may be any that keep to these rules, and one draw needn't show every extreme that they name: `channel_group`: every group 0 to 115 has exactly 128 channels.
All inputs are finite; a program needn't handle non-finite values.
Results may differ from a plain program's by a relative error of at most 0.0044.
Values may be sent and summed in bfloat16 or wider, within the bound.
A program may use at most 128 MiB of HBM per device.

v0:
```python
import jax
import jax.numpy as jnp
from jax import lax
from jax.sharding import PartitionSpec as P

D = 8192
GROUP = 128


def group_sum(channel_score, groups, count):
    onehot = (groups[:, None] == jnp.arange(count, dtype=jnp.int32)[None, :]).astype(jnp.float32)
    return jnp.dot(channel_score, onehot, precision=lax.Precision.HIGHEST) / GROUP


def shards(tokens, gate_weight, up_weight, down_weight, channel_group, owners):
    total_tokens = tokens.shape[0] * lax.axis_size("dp")
    width = gate_weight.shape[1]
    group_count = owners.shape[0]
    magnitude = jnp.sum(jnp.abs(down_weight.astype(jnp.float32)), axis=1) / D
    columns = lax.all_to_all(tokens, "dp", split_axis=1, concat_axis=0, tiled=True)
    mixed = lax.psum_scatter(
        jnp.concatenate(
            (
                jnp.dot(columns, gate_weight, preferred_element_type=jnp.float32),
                jnp.dot(columns, up_weight, preferred_element_type=jnp.float32),
            ),
            axis=1,
        ).astype(jnp.bfloat16),
        "dp",
        scatter_dimension=0,
        tiled=True,
    ).astype(jnp.float32)
    hidden = jax.nn.silu(mixed[:, :width]) * mixed[:, width:]
    energy = jnp.sum(hidden * hidden, axis=0) / total_tokens
    energy, magnitude = lax.psum((energy, magnitude), "dp")
    partial_value = group_sum(jnp.sqrt(energy) * magnitude, channel_group, group_count)
    totals = lax.psum(partial_value, "tensor")
    rank = lax.axis_index("tensor")
    row = jnp.where(owners == rank, totals, jnp.float32(0.0))
    return row[None, :]


def solution(mesh):
    return jax.shard_map(
        shards,
        mesh=mesh,
        in_specs=(
            P("dp", None),
            P("dp", "tensor"),
            P("dp", "tensor"),
            P("tensor", "dp"),
            P("tensor"),
            P(),
        ),
        out_specs=P("tensor", None),
        check_vma=False,
    )
```

profile of v0, /device:TPU:0, one launch (start us, length us, event | category | flops | bytes accessed | tf_op | source)
XLA Modules:
  0.0 162.3 jit_solution(8855123550960085499)
XLA Ops:
  6.5 0.0 reduce-scatter.2.cloned.1.call-start
  6.5 1.3 copy.11
  7.9 0.0 slice-start
  7.9 20.6 %all_to_all.19 = bf16[64,8,1024]{2,0,1:T(8,128)(2,1)S(1)} all-to-all(bf16[64,8,1024]{2,0,1:T(8,128)(2,1)S(1)} %bitcast.18), channel_id=1, replica_groups=mesh['dp'=8,'tensor'=4] {'dp'}, dimensions={1} | all-to-all | bytes 2097152 | tf_op jit(solution)/shard_map/all_to_all | solution.py:20
  28.5 0.0 slice-start.1
  28.5 9.0 %convolution_convert_fusion = bf16[512,3712]{1,0:T(8,128)(2,1)} fusion(bf16[512,1024]{1,0:T(8,128)(2,1)S(1)} %bitcast.20, bf16[1024,3712]{1,0:T(8,128)(2,1)} %param.8), kind=kOutput, calls=%fused_computation.2 | convolution fusion | flops 3894214656 | bytes 12451840 | tf_op jit(solution)/shard_map/dot_general | solution.py:25
  37.5 0.0 slice-done
  37.5 0.0 slice-done.1
  37.5 5.7 %convolution_convert_fusion.1 = bf16[512,3712]{1,0:T(8,128)(2,1)} fusion(bf16[512,1024]{1,0:T(8,128)(2,1)S(1)} %bitcast.21, bf16[1024,3712]{1,0:T(8,128)(2,1)S(1)} %bitcast.23), kind=kOutput, calls=%fused_computation.3 | convolution fusion | flops 3894214656 | bytes 12451840 | tf_op jit(solution)/shard_map/dot_general | solution.py:24
  43.2 6.8 %pad_maximum_fusion = bf16[512,7424]{1,0:T(8,128)(2,1)} fusion(bf16[512,3712]{1,0:T(8,128)(2,1)} %convolution_convert_fusion, bf16[512,3712]{1,0:T(8,128)(2,1)} %convolution_convert_fusion.1), kind=kLoop, calls=%fused_computation.1 | loop fusion | flops 15204352 | bytes 15204352 | tf_op jit(solution)/shard_map/concatenate | solution.py:22
  49.9 0.0 reduce-scatter.2.cloned.1.call-update
  50.0 0.0 copy-start.1
  50.0 0.0 copy-start
  50.0 4.7 %abs_reduce_fusion = f32[3712]{0:T(1024)S(1)} fusion(bf16[3712,1024]{1,0:T(8,128)(2,1)} %param.9), kind=kLoop, calls=%fused_computation | loop fusion | flops 11399552 | bytes 7617024 | tf_op jit(solution)/shard_map/reduce_sum | solution.py:19
  54.7 63.0 %reduce-scatter.2.cloned.1.call-done = bf16[64,7424]{1,0:T(8,128)(2,1)} async-done(((bf16[512,7424]{1,0:T(8,128)(2,1)}), bf16[64,7424]{1,0:T(8,128)(2,1)}) %reduce-scatter.2.cloned.1.call-update) | async-done | bytes 950288 | tf_op jit(solution)/shard_map/reduce_scatter | solution.py:21
  117.7 1.3 convert_element_type.8
  119.0 0.3 fusion.4
  119.3 22.9 %all-reduce = (f32[3712]{0:T(1024)S(1)}, f32[3712]{0:T(1024)S(1)}) all-reduce(f32[3712]{0:T(1024)S(1)} %get-tuple-element.7, f32[3712]{0:T(1024)S(1)} %get-tuple-element.8), channel_id=1, replica_groups=mesh['dp'=8,'tensor'=4] {'dp'}, use_global_device_ids=true, to_apply=%region_4.5 | all-reduce | flops 7424 | bytes 59392 | tf_op jit(solution)/shard_map/psum | solution.py:35
  142.3 0.0 copy-done.1
  142.3 0.9 fusion.2
  143.2 11.7 %psum.23 = f32[116]{0:T(128)S(1)} all-reduce(f32[116]{0:T(128)S(1)} %fusion.2), channel_id=1, replica_groups=mesh['dp'=8,'tensor'=4] {'tensor'}, use_global_device_ids=true, to_apply=%region_5.6 | all-reduce | flops 116 | bytes 928 | tf_op jit(solution)/shard_map/psum | solution.py:37
  154.9 0.0 copy-done
  154.9 0.5 fusion.6
  (4 shorter events, 0.0 us)
Async XLA Ops:
  6.5 111.1 %reduce-scatter.2.cloned.1.call-start = ((), (), s32[]{:S(2)}) async-start(), calls=%async_computation.2 | async-start | bytes 8552448 | tf_op jit(solution)/shard_map/reduce_scatter | solution.py:21
  7.9 29.6 %slice-start = ((s8[7602176]{0:T(1024)(128)(4,1)}), s8[4194304]{0:T(1024)(128)(4,1)S(1)}, s32[]{:S(2)}) async-start(s8[7602176]{0:T(1024)(128)(4,1)} %bitcast.22), calls=%async_computation.3 | async-start | bytes 8388608
  28.5 9.0 %slice-start.1 = ((s8[7602176]{0:T(1024)(128)(4,1)}), s8[3407872]{0:T(1024)(128)(4,1)S(1)}, s32[]{:S(2)}) async-start(s8[7602176]{0:T(1024)(128)(4,1)} %bitcast.22), calls=%async_computation.4 | async-start | bytes 6815744
  50.0 92.3 %copy-start.1 = (s32[3712]{0:T(1024)S(1)}, s32[3712]{0:T(1024)}, u32[]{:S(2)}) copy-start(s32[3712]{0:T(1024)} %param.10) | copy-start | bytes 44548
  50.0 104.9 %copy-start = (s32[116]{0:T(128)S(1)}, s32[116]{0:T(128)}, u32[]{:S(2)}) copy-start(s32[116]{0:T(128)} %param.11) | copy-start | bytes 1396
Sparse Core Ops, SparseCore 0:
  50.1 67.5 reduce-scatter.1
where the time goes:
time: 163 us; the launch traced here: 162 us
  waiting for transfers between devices  63 us (39%)
  blocking collectives  55.2 us (34%)
  matrix products  15.6 us (10%)
  other arithmetic  13.6 us (8%)
  between operations  13.5 us (8%)
    reduce_scatter x1, waiting for transfers between devices, shards(): lax.psum_scatter(jnp.concatenate((jnp.dot(columns, gate_weight, preferred...  63 us
    psum x1, blocking collectives, shards(): energy, magnitude = lax.psum((energy, magnitude), 'dp')  22.9 us
    all_to_all x1, blocking collectives, shards(): lax.all_to_all(tokens, 'dp', split_axis=1, concat_axis=0, tiled=True)  20.6 us
    psum x1, blocking collectives, shards(): totals = lax.psum(partial_value, 'tensor')  11.7 us
    dot_general x1, matrix products, shards(): jnp.dot(columns, up_weight, preferred_element_type=jnp.float32)  9 us
    concatenate x1, other arithmetic, shards(): jnp.concatenate((jnp.dot(columns, gate_weight, preferred_element_type=jnp...  6.75 us
    dot_general x1, matrix products, shards(): jnp.dot(columns, gate_weight, preferred_element_type=jnp.float32)  5.71 us
    reduce_sum x1, other arithmetic, shards(): magnitude = jnp.sum(jnp.abs(down_weight.astype(jnp.float32)), axis=1) / D  4.72 us
  transfers between devices with their start and end apart: 1, of which 1 were waited for; matrix products, arithmetic and copies ran while one was open for 3% of the time, Pallas kernels for 0%

commit v1 on v0

--- a/solution.py
+++ b/solution.py
@@ -1,10 +1,18 @@
+import functools
+
 import jax
 import jax.numpy as jnp
 from jax import lax
+from jax.experimental import pallas as pl
+from jax.experimental.pallas import tpu as pltpu
 from jax.sharding import PartitionSpec as P
 
-D = 8192
 GROUP = 128
+LANES = 128
+LAG_CORE = 2
+LAG_FIRST = 5
+LAG_SECOND = 8
+MESH = pl.DeviceIdType.MESH
 
 
 def group_sum(channel_score, groups, count):
@@ -12,11 +20,11 @@
     return jnp.dot(channel_score, onehot, precision=lax.Precision.HIGHEST) / GROUP
 
 
-def shards(tokens, gate_weight, up_weight, down_weight, channel_group, owners):
+def plain_shards(tokens, gate_weight, up_weight, down_weight, channel_group, owners):
     total_tokens = tokens.shape[0] * lax.axis_size("dp")
     width = gate_weight.shape[1]
     group_count = owners.shape[0]
-    magnitude = jnp.sum(jnp.abs(down_weight.astype(jnp.float32)), axis=1) / D
+    magnitude = jnp.sum(jnp.abs(down_weight.astype(jnp.float32)), axis=1) / tokens.shape[1]
     columns = lax.all_to_all(tokens, "dp", split_axis=1, concat_axis=0, tiled=True)
     mixed = lax.psum_scatter(
         jnp.concatenate(
@@ -40,7 +48,319 @@
     return row[None, :]
 
 
+def kernel(
+    n_tensor,
+    tok_ref,
+    gate_ref,
+    up_ref,
+    down_ref,
+    group_ref,
+    owner_ref,
+    out_ref,
+    x_buf,
+    w_buf,
+    d_buf,
+    part,
+    got_core,
+    got_first,
+    got_second,
+    energy,
+    magnitude,
+    score,
+    totals,
+    x_send,
+    x_recv,
+    local_sem,
+    g_sem,
+    u_sem,
+    d_sem,
+    core_send,
+    core_recv,
+    first_send,
+    first_recv,
+    second_send,
+    second_recv,
+    m_send,
+    m_recv,
+    e_send,
+    e_recv,
+    t_send,
+    t_recv,
+):
+    n_dp = 8
+    chunks = w_buf.shape[0]
+    block = tok_ref.shape[0]
+    depth = x_buf.shape[1]
+    me = lax.axis_index("dp")
+    z = lax.axis_index("tensor")
+    c, x, y = me % 2, (me // 2) % 2, me // 4
+    x_peer = me + 2 * (1 - 2 * x)
+    y_peer = me + 4 * (1 - 2 * y)
+    core_peer = me + (1 - 2 * c)
+    first_peer = (1 - c) * x_peer + c * y_peer
+    second_peer = (1 - c) * y_peer + c * x_peer
+
+    def peer_of(k):
+        bc, bx, by = k % 2, (k // 2) % 2, k // 4
+        return me + bc * (1 - 2 * c) + 2 * bx * (1 - 2 * x) + 4 * by * (1 - 2 * y)
+
+    def remote(src, dst, send, recv, peer):
+        return pltpu.make_async_remote_copy(
+            src_ref=src, dst_ref=dst, send_sem=send, recv_sem=recv, device_id=(peer, z), device_id_type=MESH
+        )
+
+    def gate_copy(i):
+        cols = pl.ds(pl.multiple_of(i * LANES, LANES), LANES)
+        return pltpu.make_async_copy(gate_ref.at[:, cols], w_buf.at[i, :, pl.ds(0, LANES)], g_sem.at[i])
+
+    def up_copy(i):
+        cols = pl.ds(pl.multiple_of(i * LANES, LANES), LANES)
+        return pltpu.make_async_copy(up_ref.at[:, cols], w_buf.at[i, :, pl.ds(LANES, LANES)], u_sem.at[i])
+
+    def down_copy(i):
+        rows = pl.ds(pl.multiple_of(i * LANES, LANES), LANES)
+        return pltpu.make_async_copy(down_ref.at[rows, :], d_buf.at[i], d_sem.at[i])
+
+    barrier = pltpu.get_barrier_semaphore()
+    for k in range(1, n_dp):
+        pl.semaphore_signal(barrier, inc=1, device_id=(peer_of(k), z), device_id_type=MESH)
+    for k in range(1, n_tensor):
+        pl.semaphore_signal(barrier, inc=1, device_id=(me, (z + k) % n_tensor), device_id_type=MESH)
+
+    own_cols = pl.ds(pl.multiple_of(me * depth, depth), depth)
+    own_tokens = pltpu.make_async_copy(tok_ref.at[:, own_cols], x_buf.at[pl.ds(0, block), :], local_sem)
+    own_tokens.start()
+
+    @pl.loop(0, chunks)
+    def _(i):
+        down_copy(i).start()
+
+    pl.semaphore_wait(barrier, n_dp - 1 + n_tensor - 1)
+
+    token_copies = []
+    for k in (6, 7, 2, 3, 4, 5, 1):
+        bc, bx, by = k % 2, (k // 2) % 2, k // 4
+        slot = bc * 4 + (1 - c) * (2 * bx + by) + c * (2 * by + bx)
+        peer = peer_of(k)
+        cols = pl.ds(pl.multiple_of(peer * depth, depth), depth)
+        rows = pl.ds(pl.multiple_of(slot * block, block), block)
+        copy = remote(tok_ref.at[:, cols], x_buf.at[rows, :], x_send.at[k - 1], x_recv.at[k - 1], peer)
+        copy.start()
+        token_copies.append(copy)
+
+    @pl.loop(0, chunks)
+    def _(i):
+        gate_copy(i).start()
+        up_copy(i).start()
+
+    ones = jnp.ones((8, d_buf.shape[2]), jnp.bfloat16)
+
+    @pl.loop(0, chunks)
+    def _(i):
+        down_copy(i).wait()
+        sums = lax.dot_general(
+            ones, jnp.abs(d_buf[i]), (((1,), (1,)), ((), ())), preferred_element_type=jnp.float32
+        )
+        magnitude[me, pl.ds(i, 1), :] = sums[0:1, :]
+
+    own_tokens.wait()
+    for copy in token_copies:
+        copy.wait()
+
+    m_copies = []
+    for k in range(1, n_dp):
+        copy = remote(magnitude.at[me], magnitude.at[me], m_send.at[k - 1], m_recv.at[k - 1], peer_of(k))
+        copy.start()
+        m_copies.append(copy)
+
+    half, quarter, eighth = 4 * block, 2 * block, block
+
+    def core_copy(i):
+        return remote(
+            part.at[i, pl.ds(half, half), :], got_core.at[i], core_send.at[i], core_recv.at[i], core_peer
+        )
+
+    def first_copy(i):
+        return remote(
+            part.at[i, pl.ds(quarter, quarter), :], got_first.at[i], first_send.at[i], first_recv.at[i], first_peer
+        )
+
+    def second_copy(i):
+        return remote(
+            part.at[i, pl.ds(eighth, eighth), :], got_second.at[i], second_send.at[i], second_recv.at[i], second_peer
+        )
+
+    def add(a, b):
+        return (a.astype(jnp.float32) + b.astype(jnp.float32)).astype(jnp.bfloat16)
+
+    def step(it, on):
+        after_core, after_first, after_second = it - LAG_CORE, it - LAG_FIRST, it - LAG_SECOND
+
+        @pl.when((after_core >= 0) & (after_core < chunks))
+        def _():
+            core_copy(after_core).wait_recv()
+            part[after_core, :half, :] = add(part[after_core, :half, :], got_core[after_core])
+
+        @pl.when((after_first >= 0) & (after_first < chunks))
+        def _():
+            first_copy(after_first).wait_recv()
+            part[after_first, :quarter, :] = add(part[after_first, :quarter, :], got_first[after_first])
+
+        @pl.when(it < chunks)
+        def _():
+            gate_copy(it).wait()
+            up_copy(it).wait()
+            part[it, half:, :] = jnp.dot(
+                x_buf[half:, :], w_buf[it], preferred_element_type=jnp.float32
+            ).astype(jnp.bfloat16)
+            part[it, :half, :] = jnp.dot(
+                x_buf[:half, :], w_buf[it], preferred_element_type=jnp.float32
+            ).astype(jnp.bfloat16)
+
+        @pl.when((after_first >= 0) & (after_first < chunks))
+        def _():
+            second_copy(after_first).start()
+
+        @pl.when((after_core >= 0) & (after_core < chunks))
+        def _():
+            first_copy(after_core).start()
+
+        @pl.when(it < chunks)
+        def _():
+            core_copy(it).start()
+
+        @pl.when(after_second >= 0)
+        def _():
+            second_copy(after_second).wait_recv()
+            mixed = part[after_second, :eighth, :].astype(jnp.float32) + got_second[after_second].astype(jnp.float32)
+            gate, up = mixed[:, :LANES], mixed[:, LANES:]
+            hidden = gate / (1.0 + jnp.exp(-gate)) * up
+            energy[me, pl.ds(after_second, 1), :] = jnp.sum(hidden * hidden, axis=0, keepdims=True)
+
+        return on
+
+    lax.fori_loop(0, chunks + LAG_SECOND, step, 0)
+
+    e_copies = []
+    for k in range(1, n_dp):
+        copy = remote(energy.at[me], energy.at[me], e_send.at[k - 1], e_recv.at[k - 1], peer_of(k))
+        copy.start()
+        e_copies.append(copy)
+    for copy in m_copies:
+        copy.wait()
+    mag = magnitude[0]
+    for r in range(1, n_dp):
+        mag = mag + magnitude[r]
+    mag = mag / tok_ref.shape[1]
+    for copy in e_copies:
+        copy.wait()
+    total = energy[0]
+    for r in range(1, n_dp):
+        total = total + energy[r]
+    score[...] = jnp.sqrt(total / (block * n_dp)) * mag
+
+    lines = lax.broadcasted_iota(jnp.int32, (score_groups(owner_ref), LANES), 0)
+
+    def gather(i, acc):
+        hit = lines == group_ref[pl.ds(i, 1), :]
+        return acc + jnp.where(hit, score[pl.ds(i, 1), :], 0.0)
+
+    acc = lax.fori_loop(0, chunks, gather, jnp.zeros(lines.shape, jnp.float32))
+    mine = jnp.sum(acc.T, axis=0, keepdims=True)
+    totals[z] = jnp.broadcast_to(mine, totals.shape[1:])
+    t_copies = []
+    for k in range(1, n_tensor):
+        copy = pltpu.make_async_remote_copy(
+            src_ref=totals.at[z],
+            dst_ref=totals.at[z],
+            send_sem=t_send.at[k - 1],
+            recv_sem=t_recv.at[k - 1],
+            device_id=(me, (z + k) % n_tensor),
+            device_id_type=MESH,
+        )
+        copy.start()
+        t_copies.append(copy)
+
+    @pl.loop(0, chunks)
+    def _(i):
+        core_copy(i).wait_send()
+        first_copy(i).wait_send()
+        second_copy(i).wait_send()
+
+    for copy in t_copies:
+        copy.wait()
+    row = totals[0]
+    for r in range(1, n_tensor):
+        row = row + totals[r]
+    row = row[0:1, : out_ref.shape[1]] / GROUP
+    out_ref[...] = jnp.where(owner_ref[...] == z, row, 0.0)
+
+
+def score_groups(owner_ref):
+    return -(-owner_ref.shape[1] // LANES) * LANES
+
+
+def fused_shards(n_dp, n_tensor, tokens, gate_weight, up_weight, down_weight, channel_group, owners):
+    block = tokens.shape[0]
+    depth, width = gate_weight.shape
+    chunks = width // LANES
+    count = owners.shape[0]
+    span = down_weight.shape[1]
+    rows = block * n_dp
+    vmem = pl.BlockSpec(memory_space=pltpu.VMEM)
+    hbm = pl.BlockSpec(memory_space=pl.ANY)
+    padded = -(-count // LANES) * LANES
+    dma = pltpu.SemaphoreType.DMA
+    return pl.pallas_call(
+        functools.partial(kernel, n_tensor),
+        out_shape=jax.ShapeDtypeStruct((1, count), jnp.float32),
+        in_specs=[hbm, hbm, hbm, hbm, vmem, vmem],
+        out_specs=vmem,
+        scratch_shapes=[
+            pltpu.VMEM((rows, depth), jnp.bfloat16),
+            pltpu.VMEM((chunks, depth, 2 * LANES), jnp.bfloat16),
+            pltpu.VMEM((chunks, LANES, span), jnp.bfloat16),
+            pltpu.VMEM((chunks, rows, 2 * LANES), jnp.bfloat16),
+            pltpu.VMEM((chunks, rows // 2, 2 * LANES), jnp.bfloat16),
+            pltpu.VMEM((chunks, rows // 4, 2 * LANES), jnp.bfloat16),
+            pltpu.VMEM((chunks, rows // 8, 2 * LANES), jnp.bfloat16),
+            pltpu.VMEM((n_dp, chunks, LANES), jnp.float32),
+            pltpu.VMEM((n_dp, chunks, LANES), jnp.float32),
+            pltpu.VMEM((chunks, LANES), jnp.float32),
+            pltpu.VMEM((n_tensor, 8, padded), jnp.float32),
+            dma((n_dp - 1,)),
+            dma((n_dp - 1,)),
+            dma,
+            dma((chunks,)),
+            dma((chunks,)),
+            dma((chunks,)),
+            dma((chunks,)),
+            dma((chunks,)),
+            dma((chunks,)),
+            dma((chunks,)),
+            dma((chunks,)),
+            dma((chunks,)),
+            dma((n_dp - 1,)),
+            dma((n_dp - 1,)),
+            dma((n_dp - 1,)),
+            dma((n_dp - 1,)),
+            dma((max(n_tensor - 1, 1),)),
+            dma((max(n_tensor - 1, 1),)),
+        ],
+        compiler_params=pltpu.CompilerParams(
+            collective_id=0, has_side_effects=True, vmem_limit_bytes=56 * 1024 * 1024
+        ),
+    )(tokens, gate_weight, up_weight, down_weight, channel_group.reshape(chunks, LANES), owners.reshape(1, count))
+
+
 def solution(mesh):
+    n_dp, n_tensor = mesh.shape["dp"], mesh.shape["tensor"]
+
+    def shards(tokens, gate_weight, *rest):
+        if n_dp == 8 and gate_weight.shape[1] % LANES == 0:
+            return fused_shards(n_dp, n_tensor, tokens, gate_weight, *rest)
+        return plain_shards(tokens, gate_weight, *rest)
+
     return jax.shard_map(
         shards,
         mesh=mesh,

time: 163 us -> 76.2 us (0.47)
  Pallas kernels: 0 us -> 74.7 us
  waiting for transfers between devices: 63 us -> 0 us
  blocking collectives: 55.2 us -> 0 us
  matrix products: 15.6 us -> 0 us
  other arithmetic: 13.6 us -> 0 us
  between operations: 13.5 us -> 0.01 us
    pallas_call x0 -> x1, Pallas kernels: none -> 74.7 us  [fused_shards(): pl.pallas_call(functools.partial(kernel, n_tensor), out_shape=jax.ShapeDt...]
    reduce_scatter x1 -> x0, waiting for transfers between devices: 63 us -> none  [shards(): lax.psum_scatter(jnp.concatenate((jnp.dot(columns, gate_weight, preferred...]
    psum x2 -> x0, blocking collectives: 34.6 us -> none  [the longest x1 22.9 us: shards(): energy, magnitude = lax.psum((energy, magnitude), 'dp')]
    all_to_all x1 -> x0, blocking collectives: 20.6 us -> none  [shards(): lax.all_to_all(tokens, 'dp', split_axis=1, concat_axis=0, tiled=True)]
    dot_general x3 -> x0, matrix products: 15.6 us -> none  [the longest x1 9 us: shards(): jnp.dot(columns, up_weight, preferred_element_type=jnp.float32)]
    concatenate x1 -> x0, other arithmetic: 6.75 us -> none  [shards(): jnp.concatenate((jnp.dot(columns, gate_weight, preferred_element_type=jnp...]
    reduce_sum x2 -> x0, other arithmetic: 5.01 us -> none  [the longest x1 4.72 us: shards(): magnitude = jnp.sum(jnp.abs(down_weight.astype(jnp.float32)), axis=1) / D]
  transfers between devices with their start and end apart: 1 -> 0, of which waited for: 1 -> 0; matrix products, arithmetic and copies ran while one was open for 3% -> 0% of each run, Pallas kernels for 0% -> 0%
where the time goes in v1:
time: 76.2 us; the launch traced here: 75.9 us
  Pallas kernels  74.7 us (98%)
  local copies, waits for them, and re-layouts  1.19 us (2%)
    pallas_call x1, Pallas kernels, fused_shards(): pl.pallas_call(functools.partial(kernel, n_tensor), out_shape=jax.ShapeDt...  74.7 us

profile of v1, /device:TPU:0, one launch (start us, length us, event | category | flops | bytes accessed | tf_op | source)
XLA Modules:
  0.0 75.9 jit_solution(7801787084067449537)
XLA Ops:
  0.0 74.7 %shard_map.64 = f32[1,116]{1,0:T(1,128)} custom-call(bf16[64,8192]{1,0:T(8,128)(2,1)} %tok_ref.1, bf16[1024,3712]{1,0:T(8,128)(2,1)} %gate_ref.1, bf16[1024,3712]{1,0:T(8,128)(2,1)} %up_ref.1, bf16[3712,1024]{1,0:T(8,128)(2,1)} %down_ref.1, s32[29,128]{1,0:T(8,128)} %bitcast.2, s32[1,116]{1,0:T(1,128)} %bitcast.3), custom_call_target="tpu_custom_call" | custom-call | tf_op jit(solution)/shard_map/pallas_call | solution.py:314
  74.7 1.2 %copy.8 = f32[1,116]{1,0:T(1,128)} copy(f32[1,116]{1,0:T(1,128)} %shard_map.64) | data formatting | bytes 928

commit v2 on v1

--- a/solution.py
+++ b/solution.py
@@ -9,9 +9,9 @@
 
 GROUP = 128
 LANES = 128
-LAG_CORE = 2
-LAG_FIRST = 5
-LAG_SECOND = 8
+LAG_CORE = 3
+LAG_FIRST = 8
+LAG_SECOND = 13
 MESH = pl.DeviceIdType.MESH
 
 
@@ -57,6 +57,7 @@
     group_ref,
     owner_ref,
     out_ref,
+    tok_buf,
     x_buf,
     w_buf,
     d_buf,
@@ -82,6 +83,8 @@
     second_recv,
     m_send,
     m_recv,
+    early_send,
+    early_recv,
     e_send,
     e_recv,
     t_send,
@@ -121,6 +124,8 @@
         rows = pl.ds(pl.multiple_of(i * LANES, LANES), LANES)
         return pltpu.make_async_copy(down_ref.at[rows, :], d_buf.at[i], d_sem.at[i])
 
+    load_tokens = pltpu.make_async_copy(tok_ref, tok_buf, local_sem)
+    load_tokens.start()
     barrier = pltpu.get_barrier_semaphore()
     for k in range(1, n_dp):
         pl.semaphore_signal(barrier, inc=1, device_id=(peer_of(k), z), device_id_type=MESH)
@@ -128,13 +133,12 @@
         pl.semaphore_signal(barrier, inc=1, device_id=(me, (z + k) % n_tensor), device_id_type=MESH)
 
     own_cols = pl.ds(pl.multiple_of(me * depth, depth), depth)
-    own_tokens = pltpu.make_async_copy(tok_ref.at[:, own_cols], x_buf.at[pl.ds(0, block), :], local_sem)
-    own_tokens.start()
 
     @pl.loop(0, chunks)
     def _(i):
         down_copy(i).start()
 
+    load_tokens.wait()
     pl.semaphore_wait(barrier, n_dp - 1 + n_tensor - 1)
 
     token_copies = []
@@ -144,7 +148,7 @@
         peer = peer_of(k)
         cols = pl.ds(pl.multiple_of(peer * depth, depth), depth)
         rows = pl.ds(pl.multiple_of(slot * block, block), block)
-        copy = remote(tok_ref.at[:, cols], x_buf.at[rows, :], x_send.at[k - 1], x_recv.at[k - 1], peer)
+        copy = remote(tok_buf.at[:, cols], x_buf.at[rows, :], x_send.at[k - 1], x_recv.at[k - 1], peer)
         copy.start()
         token_copies.append(copy)
 
@@ -163,7 +167,7 @@
         )
         magnitude[me, pl.ds(i, 1), :] = sums[0:1, :]
 
-    own_tokens.wait()
+    x_buf[:block, :] = tok_buf[:, own_cols]
     for copy in token_copies:
         copy.wait()
 
@@ -172,6 +176,16 @@
         copy = remote(magnitude.at[me], magnitude.at[me], m_send.at[k - 1], m_recv.at[k - 1], peer_of(k))
         copy.start()
         m_copies.append(copy)
+
+    early = (chunks - 1) // 8 * 8
+
+    def early_copy(k):
+        rows = energy.at[me, pl.ds(0, early), :]
+        return remote(rows, rows, early_send.at[k - 1], early_recv.at[k - 1], peer_of(k))
+
+    def late_copy(k):
+        rows = energy.at[me, pl.ds(early, chunks - early), :]
+        return remote(rows, rows, e_send.at[k - 1], e_recv.at[k - 1], peer_of(k))
 
     half, quarter, eighth = 4 * block, 2 * block, block
 
@@ -229,6 +243,11 @@
         def _():
             core_copy(it).start()
 
+        @pl.when(after_second == early)
+        def _():
+            for k in range(1, n_dp):
+                early_copy(k).start()
+
         @pl.when(after_second >= 0)
         def _():
             second_copy(after_second).wait_recv()
@@ -241,19 +260,17 @@
 
     lax.fori_loop(0, chunks + LAG_SECOND, step, 0)
 
-    e_copies = []
     for k in range(1, n_dp):
-        copy = remote(energy.at[me], energy.at[me], e_send.at[k - 1], e_recv.at[k - 1], peer_of(k))
-        copy.start()
-        e_copies.append(copy)
+        late_copy(k).start()
     for copy in m_copies:
         copy.wait()
     mag = magnitude[0]
     for r in range(1, n_dp):
         mag = mag + magnitude[r]
     mag = mag / tok_ref.shape[1]
-    for copy in e_copies:
-        copy.wait()
+    for k in range(1, n_dp):
+        early_copy(k).wait()
+        late_copy(k).wait_recv()
     total = energy[0]
     for r in range(1, n_dp):
         total = total + energy[r]
@@ -280,6 +297,9 @@
         )
         copy.start()
         t_copies.append(copy)
+
+    for k in range(1, n_dp):
+        late_copy(k).wait_send()
 
     @pl.loop(0, chunks)
     def _(i):
@@ -317,6 +337,7 @@
         in_specs=[hbm, hbm, hbm, hbm, vmem, vmem],
         out_specs=vmem,
         scratch_shapes=[
+            pltpu.VMEM(tokens.shape, jnp.bfloat16),
             pltpu.VMEM((rows, depth), jnp.bfloat16),
             pltpu.VMEM((chunks, depth, 2 * LANES), jnp.bfloat16),
             pltpu.VMEM((chunks, LANES, span), jnp.bfloat16),
@@ -340,6 +361,8 @@
             dma((chunks,)),
             dma((chunks,)),
             dma((chunks,)),
+            dma((n_dp - 1,)),
+            dma((n_dp - 1,)),
             dma((n_dp - 1,)),
             dma((n_dp - 1,)),
             dma((n_dp - 1,)),

time: 76.2 us -> 69.4 us (0.911)
  Pallas kernels: 74.7 us -> 68 us
    pallas_call x1, Pallas kernels: 74.7 us -> 68 us  [fused_shards(): pl.pallas_call(functools.partial(kernel, n_tensor), out_shape=jax.ShapeDt...]
where the time goes in v2:
time: 69.4 us; the launch traced here: 69.2 us
  Pallas kernels  68 us (98%)
  local copies, waits for them, and re-layouts  1.19 us (2%)
    pallas_call x1, Pallas kernels, fused_shards(): pl.pallas_call(functools.partial(kernel, n_tensor), out_shape=jax.ShapeDt...  68 us

profile of v2, /device:TPU:0, one launch (start us, length us, event | category | flops | bytes accessed | tf_op | source)
XLA Modules:
  0.0 69.2 jit_solution(10408567916213345325)
XLA Ops:
  0.0 68.0 %shard_map.64 = f32[1,116]{1,0:T(1,128)} custom-call(bf16[64,8192]{1,0:T(8,128)(2,1)} %tok_ref.1, bf16[1024,3712]{1,0:T(8,128)(2,1)} %gate_ref.1, bf16[1024,3712]{1,0:T(8,128)(2,1)} %up_ref.1, bf16[3712,1024]{1,0:T(8,128)(2,1)} %down_ref.1, s32[29,128]{1,0:T(8,128)} %bitcast.2, s32[1,116]{1,0:T(1,128)} %bitcast.3), custom_call_target="tpu_custom_call" | custom-call | tf_op jit(solution)/shard_map/pallas_call | solution.py:334
  68.0 1.2 %copy.8 = f32[1,116]{1,0:T(1,128)} copy(f32[1,116]{1,0:T(1,128)} %shard_map.64) | data formatting | bytes 928
